TPU v7x, 32 devices: a whole 2x2x4 slice. The times are simulated.
32 devices in a mesh: task: 2 (over x), ctx: 16 (over z, y, core).
Axes of the slice: x: 2, y: 2, z: 4, core: 2. Of those that a mesh axis runs over, the one named last changes fastest.
Arguments:
- base_queries: bfloat16 [2, 2048, 2048], P('task', 'ctx'), may hold values from -48 to 48
- adapter_input: bfloat16 [2, 2048, 16], P('task', 'ctx'), may hold values from -6 to 6
- adapter_up_weight: bfloat16 [2, 16, 2048], P('task'), may hold values from -1.5 to 1.5
- projected_keys: bfloat16 [2, 2048, 512], P('task', 'ctx'), may hold values from -6 to 6
- projected_values: bfloat16 [2, 2048, 512], P('task', 'ctx'), may hold values from -6 to 6
- output_gradient: bfloat16 [2, 2048, 2048], P('task', 'ctx'), may hold values from -0.52734375 to 0.52734375
- segments: int32 [2, 2048], P('task', 'ctx'), may hold values from 0 to 4, never falling along the last dimension, each value on 1 to 768 neighbouring positions
- solution: float32 [2, 32768], P('task'), may hold values from -1.5 to 1.5
- residual: float32 [2, 32768], P('task'), may hold values from -1.5 to 1.5
- direction: float32 [2, 32768], P('task'), may hold values from -1.5 to 1.5
- damping: float32 [2], P('task'), may hold values from 2 to 8
Outputs:
- new_solution: float32 [2, 32768], P('task', 'ctx')
- new_residual: float32 [2, 32768], P('task', 'ctx')
- new_direction: float32 [2, 32768], P('task', 'ctx')
- meta_gradient: float32 [32768], P('ctx')
Inputs may be any that keep to these rules, and one draw needn't show every extreme that they name: `segments`: segment numbers never fall along a task's tokens; each document holds 1 to 768 tokens, and some document holds exactly 768.
All inputs are finite; a program needn't handle non-finite values.
Results may differ from a plain program's by a relative error of at most 0.0073.
Values may be sent and summed in bfloat16 or wider, within the bound.
A program may use at most 64 MiB of HBM per device.

v0:
```python
import jax
import jax.numpy as jnp
from jax import lax
from jax.sharding import PartitionSpec as P

HEADS = 16
KV_HEADS = 4
HEAD_DIM = 128
ADAPTER_RANK = 16
SPAN = 6


def passed_along(value, axis, steps):
    count = lax.axis_size(axis)
    leading, last = (max(0, -steps), min(count, count - steps))
    return lax.ppermute(value, axis, [(source, source + steps) for source in range(leading, last)])


def attend(query_matrix, tangent_vectors, grads_in, key_window, value_window, allowed):
    per_group = HEADS // KV_HEADS
    score_scale = HEAD_DIM ** (-0.5)
    row_count = query_matrix.shape[0]
    head_parts = []
    for kv_index in range(KV_HEADS):
        low_col = kv_index * per_group * HEAD_DIM
        high_col = low_col + per_group * HEAD_DIM
        query_head = query_matrix[:, low_col:high_col].reshape(row_count, per_group, HEAD_DIM)
        tangent_head = tangent_vectors[:, low_col:high_col].reshape(row_count, per_group, HEAD_DIM)
        grad_head = grads_in[:, low_col:high_col].reshape(row_count, per_group, HEAD_DIM)
        key_head = key_window[:, kv_index * HEAD_DIM : (kv_index + 1) * HEAD_DIM]
        value_head = value_window[:, kv_index * HEAD_DIM : (kv_index + 1) * HEAD_DIM]
        scores = (
            jnp.einsum("tgd,kd->tgk", query_head, key_head, preferred_element_type=jnp.float32)
            * score_scale
        )
        slopes = (
            jnp.einsum("tgd,kd->tgk", tangent_head, key_head, preferred_element_type=jnp.float32)
            * score_scale
        )
        pulls = jnp.einsum("tgd,kd->tgk", grad_head, value_head, preferred_element_type=jnp.float32)
        key_mask = allowed[:, None, :]
        masked = jnp.where(key_mask, scores, -1e30)
        row_max = jnp.max(masked, axis=2, keepdims=True)
        exp_terms = jnp.exp(masked - row_max)
        probability = exp_terms / jnp.sum(exp_terms, axis=2, keepdims=True)
        mean_slope = jnp.sum(probability * slopes, axis=2, keepdims=True)
        mean_pull = jnp.sum(probability * pulls, axis=2, keepdims=True)
        centred = (slopes - mean_slope) * (pulls - mean_pull)
        covariance = jnp.sum(probability * centred, axis=2, keepdims=True)
        coef_rounded = (probability * (centred - covariance)).astype(jnp.bfloat16)
        head_rows = (
            jnp.einsum("tgk,kd->tgd", coef_rounded, key_head, preferred_element_type=jnp.float32)
            * score_scale
        )
        head_parts.append(head_rows.reshape(row_count, per_group * HEAD_DIM))
    return jnp.concatenate(head_parts, axis=1)


def per_device(
    base_queries,
    adapter_input,
    adapter_up_weight,
    projected_keys,
    projected_values,
    output_gradient,
    segments,
    solution,
    residual,
    direction,
    damping,
):
    tok_count = base_queries.shape[1]
    dev_index = lax.axis_index("ctx")
    adapter_rows = adapter_input[0]
    query_matrix = (
        base_queries[0].astype(jnp.float32)
        + jnp.dot(adapter_rows, adapter_up_weight[0], preferred_element_type=jnp.float32)
    ).astype(jnp.bfloat16)
    shift_matrix_fn = direction[0].reshape(ADAPTER_RANK, HEADS * HEAD_DIM)
    tangent_vectors = jnp.dot(
        adapter_rows.astype(jnp.float32), shift_matrix_fn, precision=lax.Precision.HIGHEST
    ).astype(jnp.bfloat16)
    own_block = (projected_keys[0], projected_values[0], segments[0])
    earlier = []
    for offset in range(1, SPAN + 1):
        earlier.append(passed_along((own_block[0], own_block[1], own_block[2]), "ctx", offset))
    ordered = earlier[::-1] + [own_block]
    key_window = jnp.concatenate([piece[0] for piece in ordered], axis=0)
    value_window = jnp.concatenate([piece[1] for piece in ordered], axis=0)
    seg_window = jnp.concatenate([piece[2] for piece in ordered], axis=0)
    window = (SPAN + 1) * tok_count
    key_place = dev_index * tok_count - SPAN * tok_count + jnp.arange(window, dtype=jnp.int32)
    query_place = dev_index * tok_count + jnp.arange(tok_count, dtype=jnp.int32)
    allowed = (
        (key_place[None, :] <= query_place[:, None])
        & (key_place[None, :] >= 0)
        & (seg_window[None, :] == segments[0][:, None])
    )
    curvature_product_rows = attend(
        query_matrix, tangent_vectors, output_gradient[0], key_window, value_window, allowed
    ).astype(jnp.bfloat16)
    curvature_product_term = jnp.dot(
        adapter_rows.T, curvature_product_rows, preferred_element_type=jnp.float32
    ).reshape(-1)
    damp_val = damping[0]
    dir_full = direction[0]
    res_full = residual[0]
    old_norm = jnp.sum(res_full * res_full)
    part_size = curvature_product_term.shape[0] // lax.axis_size("ctx")
    part_start = dev_index * part_size
    dir_part = lax.dynamic_slice_in_dim(dir_full, part_start, part_size, 0)
    sol_part = lax.dynamic_slice_in_dim(solution[0], part_start, part_size, 0)
    complete_curvature_product = lax.psum(curvature_product_term, "ctx")
    curved = dir_full + complete_curvature_product / damp_val
    step_len = old_norm / jnp.sum(dir_full * curved)
    res_next = res_full - step_len * curved
    ratio = jnp.sum(res_next * res_next) / old_norm
    new_residual = lax.dynamic_slice_in_dim(res_next, part_start, part_size, 0)
    new_direction = new_residual + ratio * dir_part
    new_solution = sol_part + step_len * dir_part
    meta_gradient = lax.psum(new_solution, "task") / lax.axis_size("task")
    return (new_solution[None], new_residual[None], new_direction[None], meta_gradient)


def solution(mesh):
    in_specs = (
        P("task", "ctx", None),
        P("task", "ctx", None),
        P("task", None, None),
        P("task", "ctx", None),
        P("task", "ctx", None),
        P("task", "ctx", None),
        P("task", "ctx"),
        P("task", None),
        P("task", None),
        P("task", None),
        P("task"),
    )
    out_specs = (P("task", "ctx"), P("task", "ctx"), P("task", "ctx"), P("ctx"))
    return jax.shard_map(
        per_device, mesh=mesh, in_specs=in_specs, out_specs=out_specs, check_vma=False
    )
```

profile of v0, /device:TPU:8, one launch (start us, length us, event | category | flops | bytes accessed | tf_op | source)
XLA Modules:
  0.0 247.7 jit_solution(12830081265267951997)
XLA Ops:
  7.2 4.6 %collective-permute-start = (s32[128]{0:T(128)}, s32[128]{0:T(128)S(1)}, u32[]{:S(2)}, u32[]{:S(2)}) collective-permute-start(s32[128]{0:T(128)} %bitcast.348), channel_id=1, source_target_pairs={{0,6},{1,7},{2,8},{3,9},{4,10},{5,11},{6,12},{7,13},{8,14},{9,15},... | collective-permute-start | bytes 1544 | tf_op jit(solution)/shard_map/ppermute | solution.py:16
  11.8 2.6 %collective-permute-start.1 = (s32[128]{0:T(128)}, s32[128]{0:T(128)S(1)}, u32[]{:S(2)}, u32[]{:S(2)}) collective-permute-start(s32[128]{0:T(128)} %bitcast.349), channel_id=1, source_target_pairs={{0,5},{1,6},{2,7},{3,8},{4,9},{5,10},{6,11},{7,12},{8,13},{9,14},{... | collective-permute-start | bytes 1544 | tf_op jit(solution)/shard_map/ppermute | solution.py:16
  14.5 2.8 %collective-permute-start.2 = (s32[128]{0:T(128)}, s32[128]{0:T(128)S(1)}, u32[]{:S(2)}, u32[]{:S(2)}) collective-permute-start(s32[128]{0:T(128)} %bitcast.350), channel_id=1, source_target_pairs={{0,4},{1,5},{2,6},{3,7},{4,8},{5,9},{6,10},{7,11},{8,12},{9,13},{1... | collective-permute-start | bytes 1544 | tf_op jit(solution)/shard_map/ppermute | solution.py:16
  17.2 1.9 collective-permute-start.3
  19.2 2.5 %collective-permute-start.4 = (s32[128]{0:T(128)}, s32[128]{0:T(128)S(1)}, u32[]{:S(2)}, u32[]{:S(2)}) collective-permute-start(s32[128]{0:T(128)} %bitcast.352), channel_id=1, source_target_pairs={{0,2},{1,3},{2,4},{3,5},{4,6},{5,7},{6,8},{7,9},{8,10},{9,11},{10,... | collective-permute-start | bytes 1544 | tf_op jit(solution)/shard_map/ppermute | solution.py:16
  21.8 1.4 fusion.12
  23.2 0.7 slice_bitcast_fusion.35
  24.7 0.9 reduce.3
  26.4 0.8 slice_bitcast_fusion.34
  27.8 1.9 collective-permute-start.5
  29.8 1.3 collective-permute-start.6
  31.1 1.3 collective-permute-start.7
  32.5 2.5 %collective-permute-start.8 = (bf16[128,512]{1,0:T(8,128)(2,1)S(1)}, bf16[128,512]{1,0:T(8,128)(2,1)S(1)}, u32[]{:S(2)}, u32[]{:S(2)}) collective-permute-start(bf16[128,512]{1,0:T(8,128)(2,1)S(1)} %bitcast.334), channel_id=1, source_target_pairs={{0,4},{1,5},{2,6},{3,7},{4,8},{5,9},{6,10},{7,11},{8,12},{9,13},{1... | collective-permute-start | bytes 393224 | tf_op jit(solution)/shard_map/ppermute | solution.py:16
  35.0 3.1 %collective-permute-start.9 = (bf16[128,512]{1,0:T(8,128)(2,1)S(1)}, bf16[128,512]{1,0:T(8,128)(2,1)S(1)}, u32[]{:S(2)}, u32[]{:S(2)}) collective-permute-start(bf16[128,512]{1,0:T(8,128)(2,1)S(1)} %bitcast.335), channel_id=1, source_target_pairs={{0,3},{1,4},{2,5},{3,6},{4,7},{5,8},{6,9},{7,10},{8,11},{9,12},{10... | collective-permute-start | bytes 393224 | tf_op jit(solution)/shard_map/ppermute | solution.py:16
  38.2 2.2 collective-permute-start.10
  40.6 2.1 collective-permute-start.11
  42.7 1.3 collective-permute-start.12
  44.1 1.3 collective-permute-start.13
  45.4 3.8 %collective-permute-start.14 = (bf16[128,512]{1,0:T(8,128)(2,1)S(1)}, bf16[128,512]{1,0:T(8,128)(2,1)S(1)}, u32[]{:S(2)}, u32[]{:S(2)}) collective-permute-start(bf16[128,512]{1,0:T(8,128)(2,1)S(1)} %bitcast.340), channel_id=1, source_target_pairs={{0,4},{1,5},{2,6},{3,7},{4,8},{5,9},{6,10},{7,11},{8,12},{9,13},{1... | collective-permute-start | bytes 393224 | tf_op jit(solution)/shard_map/ppermute | solution.py:16
  49.2 4.9 %collective-permute-start.15 = (bf16[128,512]{1,0:T(8,128)(2,1)S(1)}, bf16[128,512]{1,0:T(8,128)(2,1)S(1)}, u32[]{:S(2)}, u32[]{:S(2)}) collective-permute-start(bf16[128,512]{1,0:T(8,128)(2,1)S(1)} %bitcast.341), channel_id=1, source_target_pairs={{0,3},{1,4},{2,5},{3,6},{4,7},{5,8},{6,9},{7,10},{8,11},{9,12},{10... | collective-permute-start | bytes 393224 | tf_op jit(solution)/shard_map/ppermute | solution.py:16
  54.1 5.8 %collective-permute-start.16 = (bf16[128,512]{1,0:T(8,128)(2,1)S(1)}, bf16[128,512]{1,0:T(8,128)(2,1)S(1)}, u32[]{:S(2)}, u32[]{:S(2)}) collective-permute-start(bf16[128,512]{1,0:T(8,128)(2,1)S(1)} %bitcast.342), channel_id=1, source_target_pairs={{0,2},{1,3},{2,4},{3,5},{4,6},{5,7},{6,8},{7,9},{8,10},{9,11},{10,... | collective-permute-start | bytes 393224 | tf_op jit(solution)/shard_map/ppermute | solution.py:16
  60.0 4.2 %collective-permute-start.17 = (bf16[128,512]{1,0:T(8,128)(2,1)S(1)}, bf16[128,512]{1,0:T(8,128)(2,1)S(1)}, u32[]{:S(2)}, u32[]{:S(2)}) collective-permute-start(bf16[128,512]{1,0:T(8,128)(2,1)S(1)} %bitcast.343), channel_id=1, source_target_pairs={{0,1},{1,2},{2,3},{3,4},{4,5},{5,6},{6,7},{7,8},{8,9},{9,10},{10,1... | collective-permute-start | bytes 393224 | tf_op jit(solution)/shard_map/ppermute | solution.py:16
  64.3 4.6 %collective-permute-done.17 = bf16[128,512]{1,0:T(8,128)(2,1)S(1)} collective-permute-done((bf16[128,512]{1,0:T(8,128)(2,1)S(1)}, bf16[128,512]{1,0:T(8,128)(2,1)S(1)}, u32[]{:S(2)}, u32[]{:S(2)}) %collective-permute-start.17) | collective-permute-done | bytes 131104 | tf_op jit(solution)/shard_map/ppermute | solution.py:16
  69.0 3.1 %fusion.228 = (f32[128,4]{0,1:T(4,128)S(1)}, f32[128,4,896]{2,0,1:T(8,128)}) fusion(pred[128,896]{1,0:T(8,128)(4,1)S(1)} %compare_and_fusion, bf16[16,4,8,128]{3,2,1,0:T(8,128)(2,1)S(1)} %copy-done.11, bf16[896,512]{1,0:T(8,128)(2,1)} %copy-done.15), kind=kOutput, calls=%fused_computation.226 | convolution fusion | flops 119276416 | bytes 2312192 | tf_op jit(solution)/shard_map/sub | solution.py:44
  72.1 2.1 fusion.221
  74.2 1.7 fusion.75
  75.9 1.8 fusion.74
  77.6 2.1 fusion.214
  79.7 1.7 fusion.73
  81.4 2.1 fusion.207
  83.9 3.4 %fusion.9 = f32[128,4,896]{2,0,1:T(8,128)} fusion(bf16[128,4,128]{0,2,1:T(8,128)(2,1)S(1)} %bitcast.331, bf16[896,512]{1,0:T(8,128)(2,1)S(1)} %constant_dynamic-update-slice_fusion.8, f32[128,4,896]{2,0,1:T(8,128)} %get-tuple-element.35, f32[128,4]{0,1:T(4,128)S(1)} %get-tuple-element.34), kind=kOutput, calls=%fused_computation.9 | convolution fusion | flops 118359424 | bytes 4032512 | tf_op jit(solution)/shard_map/sub | solution.py:48
  87.3 5.7 %multiply_reduce_fusion.6 = (f32[128,4]{0,1:T(4,128)S(1)}, f32[128,4,896]{2,0,1:T(8,128)}) fusion(f32[128,4,896]{2,0,1:T(8,128)} %get-tuple-element.35, f32[128,4]{0,1:T(4,128)S(1)} %get-tuple-element.34, f32[128,4,896]{2,0,1:T(8,128)} %fusion.9, f32[896,128,4]{0,1,2:T(8,128)} %fusion.75, bf16[16,4,8,128]{3,2,1,0:T(8,128)(2,1)} %get-tuple-element.8, ...), kind=kOutput, calls=%fused_computation.46 | convolution fusion | flops 239469440 | bytes 9902080 | tf_op jit(solution)/shard_map/sub | solution.py:48
  93.0 3.8 %fusion.37 = bf16[128,4,128]{0,2,1:T(8,128)(2,1)} fusion(f32[128,4,896]{2,0,1:T(8,128)} %get-tuple-element.37, f32[128,4]{0,1:T(4,128)S(1)} %get-tuple-element.36, bf16[896,512]{1,0:T(8,128)(2,1)} %copy-done.15, f32[128,4]{0,1:T(4,128)S(1)} %get-tuple-element.34, pred[128,896]{1,0:T(8,128)(4,1)} %copy-done.13, bf16[16,4,8,128]{3,2,1,0:T(8,128)(2,1)} %get-tuple-element.12), kind=kOutput, calls=%fused_computation.63 | convolution fusion | flops 238224768 | bytes 2674688 | tf_op jit(solution)/shard_map/tgk,kd->tgd/dot_general | solution.py:52
  96.8 3.4 %fusion.6 = f32[128,4,896]{2,0,1:T(8,128)} fusion(bf16[128,4,128]{0,2,1:T(8,128)(2,1)S(1)} %bitcast.329, bf16[896,512]{1,0:T(8,128)(2,1)S(1)} %constant_dynamic-update-slice_fusion.8, f32[128,4,896]{2,0,1:T(8,128)} %get-tuple-element.31, f32[128,4]{0,1:T(4,128)S(1)} %get-tuple-element.30), kind=kOutput, calls=%fused_computation.6 | convolution fusion | flops 118359424 | bytes 4032512 | tf_op jit(solution)/shard_map/sub | solution.py:48
  100.2 5.6 %multiply_reduce_fusion.4 = (f32[128,4]{0,1:T(4,128)S(1)}, f32[128,4,896]{2,0,1:T(8,128)}) fusion(f32[128,4,896]{2,0,1:T(8,128)} %get-tuple-element.31, f32[128,4]{0,1:T(4,128)S(1)} %get-tuple-element.30, f32[128,4,896]{2,0,1:T(8,128)} %fusion.6, f32[896,128,4]{0,1,2:T(8,128)} %fusion.74, bf16[16,4,8,128]{3,2,1,0:T(8,128)(2,1)S(1)} %copy-done.12, ...), kind=kOutput, calls=%fused_computation.40 | convolution fusion | flops 239469440 | bytes 9902080 | tf_op jit(solution)/shard_map/sub | solution.py:48
  105.8 3.2 %fusion.38 = bf16[128,4,128]{0,2,1:T(8,128)(2,1)S(1)} fusion(f32[128,4,896]{2,0,1:T(8,128)} %get-tuple-element.33, f32[128,4]{0,1:T(4,128)S(1)} %get-tuple-element.32, bf16[896,512]{1,0:T(8,128)(2,1)} %copy-done.15, f32[128,4]{0,1:T(4,128)S(1)} %get-tuple-element.30, pred[128,896]{1,0:T(8,128)(4,1)} %copy-done.13, bf16[16,4,8,128]{3,2,1,0:T(8,128)(2,1)} %copy-done.9), kind=kOutput, calls=%fused_computation.64 | convolution fusion | flops 238224768 | bytes 2674688 | tf_op jit(solution)/shard_map/tgk,kd->tgd/dot_general | solution.py:52
  109.0 3.4 %fusion.3 = f32[128,4,896]{2,0,1:T(8,128)} fusion(bf16[128,4,128]{0,2,1:T(8,128)(2,1)S(1)} %bitcast.327, bf16[896,512]{1,0:T(8,128)(2,1)S(1)} %constant_dynamic-update-slice_fusion.8, f32[128,4,896]{2,0,1:T(8,128)} %get-tuple-element.27, f32[128,4]{0,1:T(4,128)S(1)} %get-tuple-element.26), kind=kOutput, calls=%fused_computation.3 | convolution fusion | flops 118359424 | bytes 4032512 | tf_op jit(solution)/shard_map/sub | solution.py:48
  112.4 5.8 %multiply_reduce_fusion.2 = (f32[128,4]{0,1:T(4,128)S(1)}, f32[128,4,896]{2,0,1:T(8,128)}) fusion(f32[128,4,896]{2,0,1:T(8,128)} %get-tuple-element.27, f32[128,4]{0,1:T(4,128)S(1)} %get-tuple-element.26, f32[128,4,896]{2,0,1:T(8,128)} %fusion.3, f32[896,128,4]{0,1,2:T(8,128)} %fusion.73, bf16[16,4,8,128]{3,2,1,0:T(8,128)(2,1)S(1)} %copy-done.10, ...), kind=kOutput, calls=%fused_computation.34 | convolution fusion | flops 239469440 | bytes 9902080 | tf_op jit(solution)/shard_map/sub | solution.py:48
  118.2 3.2 %fusion.39 = bf16[128,4,128]{0,2,1:T(8,128)(2,1)S(1)} fusion(f32[128,4,896]{2,0,1:T(8,128)} %get-tuple-element.29, f32[128,4]{0,1:T(4,128)S(1)} %get-tuple-element.28, bf16[896,512]{1,0:T(8,128)(2,1)} %copy-done.15, f32[128,4]{0,1:T(4,128)S(1)} %get-tuple-element.26, pred[128,896]{1,0:T(8,128)(4,1)} %copy-done.13, bf16[16,4,8,128]{3,2,1,0:T(8,128)(2,1)} %copy-done.7), kind=kOutput, calls=%fused_computation.65 | convolution fusion | flops 238224768 | bytes 2674688 | tf_op jit(solution)/shard_map/tgk,kd->tgd/dot_general | solution.py:52
  121.4 3.3 %fusion = f32[128,4,896]{2,0,1:T(8,128)} fusion(bf16[128,4,128]{0,2,1:T(8,128)(2,1)S(1)} %bitcast.325, bf16[896,512]{1,0:T(8,128)(2,1)S(1)} %constant_dynamic-update-slice_fusion.8, f32[128,4,896]{2,0,1:T(8,128)} %get-tuple-element.23, f32[128,4]{0,1:T(4,128)S(1)} %get-tuple-element.22), kind=kOutput, calls=%fused_computation | convolution fusion | flops 118359424 | bytes 4032512 | tf_op jit(solution)/shard_map/sub | solution.py:48
  124.8 5.1 %multiply_reduce_fusion = (f32[128,4]{0,1:T(4,128)S(1)}, f32[128,4,896]{2,0,1:T(8,128)}) fusion(f32[128,4,896]{2,0,1:T(8,128)} %get-tuple-element.23, f32[128,4]{0,1:T(4,128)S(1)} %get-tuple-element.22, f32[128,4,896]{2,0,1:T(8,128)} %fusion, f32[896,128,4]{0,1,2:T(8,128)S(1)} %fusion.72, bf16[16,4,8,128]{3,2,1,0:T(8,128)(2,1)S(1)} %copy-done.8, ...), kind=kOutput, calls=%fused_computation.28 | convolution fusion | flops 239469440 | bytes 9902080 | tf_op jit(solution)/shard_map/sub | solution.py:48
  129.9 3.2 %fusion.40 = bf16[128,4,128]{0,2,1:T(8,128)(2,1)S(1)} fusion(f32[128,4,896]{2,0,1:T(8,128)} %get-tuple-element.25, f32[128,4]{0,1:T(4,128)S(1)} %get-tuple-element.24, bf16[896,512]{1,0:T(8,128)(2,1)S(1)} %copy-done.17, f32[128,4]{0,1:T(4,128)S(1)} %get-tuple-element.22, pred[128,896]{1,0:T(8,128)(4,1)} %copy-done.13, bf16[16,4,8,128]{3,2,1,0:T(8,128)(2,1)} %copy-done.6), kind=kOutput, calls=%fused_computation.66 | convolution fusion | flops 238224768 | bytes 2674688 | tf_op jit(solution)/shard_map/tgk,kd->tgd/dot_general | solution.py:52
  133.3 0.7 copy.76
  134.6 93.5 %all-reduce.2.cloned.1.call-done = f32[32768]{0:T(1024)} async-done(((f32[32768]{0:T(1024)}), f32[32768]{0:T(1024)}) %all-reduce.2.cloned.1.call-update) | async-done | bytes 131088 | tf_op jit(solution)/shard_map/psum | solution.py:113
  228.1 1.5 multiply_reduce_fusion.9
  231.0 1.6 multiply_reduce_fusion.8
  233.9 0.7 broadcast_multiply_fusion.1
  234.6 5.0 %psum.15 = f32[2048]{0:T(1024)S(1)} all-reduce(f32[2048]{0:T(1024)S(1)} %bitcast.344), channel_id=1, replica_groups=mesh['task'=2,'ctx'=16] {'task'}, use_global_device_ids=true, to_apply=%region_24.25 | all-reduce | flops 2048 | bytes 16384 | tf_op jit(solution)/shard_map/psum | solution.py:121
  (97 shorter events, 4.6 us)
Async XLA Ops:
  7.2 14.6 %copy-start = (bf16[1,16,2048]{2,1,0:T(8,128)(2,1)S(1)}, bf16[1,16,2048]{2,1,0:T(8,128)(2,1)}, u32[]{:S(2)}) copy-start(bf16[1,16,2048]{2,1,0:T(8,128)(2,1)} %param.13) | copy-start | bytes 196612
  7.2 16.7 %copy-start.3 = (bf16[1,128,2048]{2,1,0:T(8,128)(2,1)S(1)}, bf16[1,128,2048]{2,1,0:T(8,128)(2,1)}, u32[]{:S(2)}) copy-start(bf16[1,128,2048]{2,1,0:T(8,128)(2,1)} %param.16) | copy-start | bytes 1572868
  7.2 220.9 %all-reduce.2.cloned.1.call-start = ((), (), s32[]{:S(2)}) async-start(), calls=%async_computation | async-start | bytes 262144 | tf_op jit(solution)/shard_map/psum | solution.py:113
  7.2 20.6 %collective-permute-start = (s32[128]{0:T(128)}, s32[128]{0:T(128)S(1)}, u32[]{:S(2)}, u32[]{:S(2)}) collective-permute-start(s32[128]{0:T(128)} %bitcast.348), channel_id=1, source_target_pairs={{0,6},{1,7},{2,8},{3,9},{4,10},{5,11},{6,12},{7,13},{8,14},{9,15},... | collective-permute-start | bytes 1544 | tf_op jit(solution)/shard_map/ppermute | solution.py:16
  11.8 18.0 %collective-permute-start.1 = (s32[128]{0:T(128)}, s32[128]{0:T(128)S(1)}, u32[]{:S(2)}, u32[]{:S(2)}) collective-permute-start(s32[128]{0:T(128)} %bitcast.349), channel_id=1, source_target_pairs={{0,5},{1,6},{2,7},{3,8},{4,9},{5,10},{6,11},{7,12},{8,13},{9,14},{... | collective-permute-start | bytes 1544 | tf_op jit(solution)/shard_map/ppermute | solution.py:16
  14.5 16.7 %collective-permute-start.2 = (s32[128]{0:T(128)}, s32[128]{0:T(128)S(1)}, u32[]{:S(2)}, u32[]{:S(2)}) collective-permute-start(s32[128]{0:T(128)} %bitcast.350), channel_id=1, source_target_pairs={{0,4},{1,5},{2,6},{3,7},{4,8},{5,9},{6,10},{7,11},{8,12},{9,13},{1... | collective-permute-start | bytes 1544 | tf_op jit(solution)/shard_map/ppermute | solution.py:16
  17.2 15.2 %collective-permute-start.3 = (s32[128]{0:T(128)}, s32[128]{0:T(128)S(1)}, u32[]{:S(2)}, u32[]{:S(2)}) collective-permute-start(s32[128]{0:T(128)} %bitcast.351), channel_id=1, source_target_pairs={{0,3},{1,4},{2,5},{3,6},{4,7},{5,8},{6,9},{7,10},{8,11},{9,12},{10... | collective-permute-start | bytes 1544 | tf_op jit(solution)/shard_map/ppermute | solution.py:16
  19.2 15.9 %collective-permute-start.4 = (s32[128]{0:T(128)}, s32[128]{0:T(128)S(1)}, u32[]{:S(2)}, u32[]{:S(2)}) collective-permute-start(s32[128]{0:T(128)} %bitcast.352), channel_id=1, source_target_pairs={{0,2},{1,3},{2,4},{3,5},{4,6},{5,7},{6,8},{7,9},{8,10},{9,11},{10,... | collective-permute-start | bytes 1544 | tf_op jit(solution)/shard_map/ppermute | solution.py:16
  23.2 1.6 copy-start.1
  23.2 2.6 %copy-start.18 = (bf16[1,128,16]{1,2,0:T(8,128)(2,1)S(1)}, bf16[1,128,16]{1,2,0:T(8,128)(2,1)}, u32[]{:S(2)}) copy-start(bf16[1,128,16]{1,2,0:T(8,128)(2,1)} %param.12) | copy-start | bytes 12292
  23.9 48.2 %copy-start.9 = (bf16[16,4,8,128]{3,2,1,0:T(8,128)(2,1)}, bf16[16,4,8,128]{3,2,1,0:T(8,128)(2,1)S(1)}, u32[]{:S(2)}) copy-start(bf16[16,4,8,128]{3,2,1,0:T(8,128)(2,1)S(1)} %get-tuple-element.15) | copy-start | bytes 393220
  23.9 53.8 %copy-start.7 = (bf16[16,4,8,128]{3,2,1,0:T(8,128)(2,1)}, bf16[16,4,8,128]{3,2,1,0:T(8,128)(2,1)S(1)}, u32[]{:S(2)}) copy-start(bf16[16,4,8,128]{3,2,1,0:T(8,128)(2,1)S(1)} %get-tuple-element.14) | copy-start | bytes 393220
  23.9 57.5 %copy-start.6 = (bf16[16,4,8,128]{3,2,1,0:T(8,128)(2,1)}, bf16[16,4,8,128]{3,2,1,0:T(8,128)(2,1)S(1)}, u32[]{:S(2)}) copy-start(bf16[16,4,8,128]{3,2,1,0:T(8,128)(2,1)S(1)} %get-tuple-element.13) | copy-start | bytes 393220
  24.1 3.7 %copy-start.19 = (s32[1,128]{1,0:T(1,128)S(1)}, s32[1,128]{1,0:T(1,128)}, u32[]{:S(2)}) copy-start(s32[1,128]{1,0:T(1,128)} %param.17) | copy-start | bytes 1540
  24.2 5.6 %copy-start.4 = (bf16[1,128,512]{2,1,0:T(8,128)(2,1)S(1)}, bf16[1,128,512]{2,1,0:T(8,128)(2,1)}, u32[]{:S(2)}) copy-start(bf16[1,128,512]{2,1,0:T(8,128)(2,1)} %param.14) | copy-start | bytes 393220
  24.2 18.6 %copy-start.5 = (bf16[1,128,512]{2,1,0:T(8,128)(2,1)S(1)}, bf16[1,128,512]{2,1,0:T(8,128)(2,1)}, u32[]{:S(2)}) copy-start(bf16[1,128,512]{2,1,0:T(8,128)(2,1)} %param.15) | copy-start | bytes 393220
  27.8 10.3 %collective-permute-start.5 = (s32[128]{0:T(128)S(1)}, s32[128]{0:T(128)S(1)}, u32[]{:S(2)}, u32[]{:S(2)}) collective-permute-start(s32[128]{0:T(128)S(1)} %bitcast.353), channel_id=1, source_target_pairs={{0,1},{1,2},{2,3},{3,4},{4,5},{5,6},{6,7},{7,8},{8,9},{9,10},{10,1... | collective-permute-start | bytes 1544 | tf_op jit(solution)/shard_map/ppermute | solution.py:16
  29.8 10.8 %collective-permute-start.6 = (bf16[128,512]{1,0:T(8,128)(2,1)S(1)}, bf16[128,512]{1,0:T(8,128)(2,1)S(1)}, u32[]{:S(2)}, u32[]{:S(2)}) collective-permute-start(bf16[128,512]{1,0:T(8,128)(2,1)S(1)} %bitcast.332), channel_id=1, source_target_pairs={{0,6},{1,7},{2,8},{3,9},{4,10},{5,11},{6,12},{7,13},{8,14},{9,15},... | collective-permute-start | bytes 393224 | tf_op jit(solution)/shard_map/ppermute | solution.py:16
  31.1 11.6 %collective-permute-start.7 = (bf16[128,512]{1,0:T(8,128)(2,1)S(1)}, bf16[128,512]{1,0:T(8,128)(2,1)S(1)}, u32[]{:S(2)}, u32[]{:S(2)}) collective-permute-start(bf16[128,512]{1,0:T(8,128)(2,1)S(1)} %bitcast.333), channel_id=1, source_target_pairs={{0,5},{1,6},{2,7},{3,8},{4,9},{5,10},{6,11},{7,12},{8,13},{9,14},{... | collective-permute-start | bytes 393224 | tf_op jit(solution)/shard_map/ppermute | solution.py:16
  32.5 11.6 %collective-permute-start.8 = (bf16[128,512]{1,0:T(8,128)(2,1)S(1)}, bf16[128,512]{1,0:T(8,128)(2,1)S(1)}, u32[]{:S(2)}, u32[]{:S(2)}) collective-permute-start(bf16[128,512]{1,0:T(8,128)(2,1)S(1)} %bitcast.334), channel_id=1, source_target_pairs={{0,4},{1,5},{2,6},{3,7},{4,8},{5,9},{6,10},{7,11},{8,12},{9,13},{1... | collective-permute-start | bytes 393224 | tf_op jit(solution)/shard_map/ppermute | solution.py:16
  35.0 10.4 %collective-permute-start.9 = (bf16[128,512]{1,0:T(8,128)(2,1)S(1)}, bf16[128,512]{1,0:T(8,128)(2,1)S(1)}, u32[]{:S(2)}, u32[]{:S(2)}) collective-permute-start(bf16[128,512]{1,0:T(8,128)(2,1)S(1)} %bitcast.335), channel_id=1, source_target_pairs={{0,3},{1,4},{2,5},{3,6},{4,7},{5,8},{6,9},{7,10},{8,11},{9,12},{10... | collective-permute-start | bytes 393224 | tf_op jit(solution)/shard_map/ppermute | solution.py:16
  38.2 11.0 %collective-permute-start.10 = (bf16[128,512]{1,0:T(8,128)(2,1)S(1)}, bf16[128,512]{1,0:T(8,128)(2,1)S(1)}, u32[]{:S(2)}, u32[]{:S(2)}) collective-permute-start(bf16[128,512]{1,0:T(8,128)(2,1)S(1)} %bitcast.336), channel_id=1, source_target_pairs={{0,2},{1,3},{2,4},{3,5},{4,6},{5,7},{6,8},{7,9},{8,10},{9,11},{10,... | collective-permute-start | bytes 393224 | tf_op jit(solution)/shard_map/ppermute | solution.py:16
  40.6 40.8 %copy-start.13 = (pred[128,896]{1,0:T(8,128)(4,1)}, pred[128,896]{1,0:T(8,128)(4,1)S(1)}, u32[]{:S(2)}) copy-start(pred[128,896]{1,0:T(8,128)(4,1)S(1)} %compare_and_fusion) | copy-start | bytes 344068
  40.6 28.3 %copy-start.11 = (bf16[16,4,8,128]{3,2,1,0:T(8,128)(2,1)S(1)}, bf16[16,4,8,128]{3,2,1,0:T(8,128)(2,1)}, u32[]{:S(2)}) copy-start(bf16[16,4,8,128]{3,2,1,0:T(8,128)(2,1)} %get-tuple-element.12) | copy-start | bytes 393220
  40.6 13.5 %collective-permute-start.11 = (bf16[128,512]{1,0:T(8,128)(2,1)S(1)}, bf16[128,512]{1,0:T(8,128)(2,1)S(1)}, u32[]{:S(2)}, u32[]{:S(2)}) collective-permute-start(bf16[128,512]{1,0:T(8,128)(2,1)S(1)} %bitcast.337), channel_id=1, source_target_pairs={{0,1},{1,2},{2,3},{3,4},{4,5},{5,6},{6,7},{7,8},{8,9},{9,10},{10,1... | collective-permute-start | bytes 393224 | tf_op jit(solution)/shard_map/ppermute | solution.py:16
  42.7 17.3 %collective-permute-start.12 = (bf16[128,512]{1,0:T(8,128)(2,1)S(1)}, bf16[128,512]{1,0:T(8,128)(2,1)S(1)}, u32[]{:S(2)}, u32[]{:S(2)}) collective-permute-start(bf16[128,512]{1,0:T(8,128)(2,1)S(1)} %bitcast.338), channel_id=1, source_target_pairs={{0,6},{1,7},{2,8},{3,9},{4,10},{5,11},{6,12},{7,13},{8,14},{9,15},... | collective-permute-start | bytes 393224 | tf_op jit(solution)/shard_map/ppermute | solution.py:16
  44.1 20.2 %collective-permute-start.13 = (bf16[128,512]{1,0:T(8,128)(2,1)S(1)}, bf16[128,512]{1,0:T(8,128)(2,1)S(1)}, u32[]{:S(2)}, u32[]{:S(2)}) collective-permute-start(bf16[128,512]{1,0:T(8,128)(2,1)S(1)} %bitcast.339), channel_id=1, source_target_pairs={{0,5},{1,6},{2,7},{3,8},{4,9},{5,10},{6,11},{7,12},{8,13},{9,14},{... | collective-permute-start | bytes 393224 | tf_op jit(solution)/shard_map/ppermute | solution.py:16
  45.4 18.9 %collective-permute-start.14 = (bf16[128,512]{1,0:T(8,128)(2,1)S(1)}, bf16[128,512]{1,0:T(8,128)(2,1)S(1)}, u32[]{:S(2)}, u32[]{:S(2)}) collective-permute-start(bf16[128,512]{1,0:T(8,128)(2,1)S(1)} %bitcast.340), channel_id=1, source_target_pairs={{0,4},{1,5},{2,6},{3,7},{4,8},{5,9},{6,10},{7,11},{8,12},{9,13},{1... | collective-permute-start | bytes 393224 | tf_op jit(solution)/shard_map/ppermute | solution.py:16
  49.2 15.1 %collective-permute-start.15 = (bf16[128,512]{1,0:T(8,128)(2,1)S(1)}, bf16[128,512]{1,0:T(8,128)(2,1)S(1)}, u32[]{:S(2)}, u32[]{:S(2)}) collective-permute-start(bf16[128,512]{1,0:T(8,128)(2,1)S(1)} %bitcast.341), channel_id=1, source_target_pairs={{0,3},{1,4},{2,5},{3,6},{4,7},{5,8},{6,9},{7,10},{8,11},{9,12},{10... | collective-permute-start | bytes 393224 | tf_op jit(solution)/shard_map/ppermute | solution.py:16
  54.1 10.2 %collective-permute-start.16 = (bf16[128,512]{1,0:T(8,128)(2,1)S(1)}, bf16[128,512]{1,0:T(8,128)(2,1)S(1)}, u32[]{:S(2)}, u32[]{:S(2)}) collective-permute-start(bf16[128,512]{1,0:T(8,128)(2,1)S(1)} %bitcast.342), channel_id=1, source_target_pairs={{0,2},{1,3},{2,4},{3,5},{4,6},{5,7},{6,8},{7,9},{8,10},{9,11},{10,... | collective-permute-start | bytes 393224 | tf_op jit(solution)/shard_map/ppermute | solution.py:16
  60.0 9.0 %copy-start.15 = (bf16[896,512]{1,0:T(8,128)(2,1)}, bf16[896,512]{1,0:T(8,128)(2,1)S(1)}, u32[]{:S(2)}) copy-start(bf16[896,512]{1,0:T(8,128)(2,1)S(1)} %constant_dynamic-update-slice_fusion.1) | copy-start | bytes 2752516
  60.0 8.9 %collective-permute-start.17 = (bf16[128,512]{1,0:T(8,128)(2,1)S(1)}, bf16[128,512]{1,0:T(8,128)(2,1)S(1)}, u32[]{:S(2)}, u32[]{:S(2)}) collective-permute-start(bf16[128,512]{1,0:T(8,128)(2,1)S(1)} %bitcast.343), channel_id=1, source_target_pairs={{0,1},{1,2},{2,3},{3,4},{4,5},{5,6},{6,7},{7,8},{8,9},{9,10},{10,1... | collective-permute-start | bytes 393224 | tf_op jit(solution)/shard_map/ppermute | solution.py:16
  69.0 3.1 %copy-start.16 = (bf16[896,512]{1,0:T(8,128)(2,1)S(1)}, bf16[896,512]{1,0:T(8,128)(2,1)}, u32[]{:S(2)}) copy-start(bf16[896,512]{1,0:T(8,128)(2,1)} %copy-done.15) | copy-start | bytes 2752516
  96.8 3.4 %copy-start.12 = (bf16[16,4,8,128]{3,2,1,0:T(8,128)(2,1)S(1)}, bf16[16,4,8,128]{3,2,1,0:T(8,128)(2,1)}, u32[]{:S(2)}) copy-start(bf16[16,4,8,128]{3,2,1,0:T(8,128)(2,1)} %get-tuple-element.11) | copy-start | bytes 393220
  109.0 3.4 %copy-start.10 = (bf16[16,4,8,128]{3,2,1,0:T(8,128)(2,1)S(1)}, bf16[16,4,8,128]{3,2,1,0:T(8,128)(2,1)}, u32[]{:S(2)}) copy-start(bf16[16,4,8,128]{3,2,1,0:T(8,128)(2,1)} %get-tuple-element.10) | copy-start | bytes 393220
  121.4 3.4 %copy-start.8 = (bf16[16,4,8,128]{3,2,1,0:T(8,128)(2,1)S(1)}, bf16[16,4,8,128]{3,2,1,0:T(8,128)(2,1)}, u32[]{:S(2)}) copy-start(bf16[16,4,8,128]{3,2,1,0:T(8,128)(2,1)} %get-tuple-element.9) | copy-start | bytes 393220
  124.8 5.1 %copy-start.17 = (bf16[896,512]{1,0:T(8,128)(2,1)S(1)}, bf16[896,512]{1,0:T(8,128)(2,1)}, u32[]{:S(2)}) copy-start(bf16[896,512]{1,0:T(8,128)(2,1)} %copy-done.15) | copy-start | bytes 2752516
  129.8 3.2 %copy-start.20 = (bf16[128,4,128]{0,2,1:T(8,128)(2,1)S(1)}, bf16[128,4,128]{0,2,1:T(8,128)(2,1)}, u32[]{:S(2)}) copy-start(bf16[128,4,128]{0,2,1:T(8,128)(2,1)} %fusion.37) | copy-start | bytes 393220
  133.0 1.0 copy-start.2
  234.6 6.2 %copy-start.14 = (f32[1,2048]{1,0:T(1,128)}, f32[1,2048]{1,0:T(1,128)S(1)}, u32[]{:S(2)}) copy-start(f32[1,2048]{1,0:T(1,128)S(1)} %get-tuple-element.21) | copy-start | bytes 24580
Sparse Core Ops, SparseCore 0:
  134.1 93.9 all-reduce.1
where the time goes:
time: 249 us; the launch traced here: 248 us
  waiting for transfers between devices  98.1 us (39%)
  matrix products  66.2 us (27%)
  starting transfers between devices  50.1 us (20%)
  between operations  18.1 us (7%)
  other arithmetic  6.81 us (3%)
  blocking collectives  5 us (2%)
  local copies, waits for them, and re-layouts  3.33 us (1%)
    psum x1, waiting for transfers between devices, per_device(): complete_curvature_product = lax.psum(curvature_product_term, 'ctx')  93.5 us
    ppermute x18, starting transfers between devices, passed_along(): lax.ppermute(value, axis, [(source, source + steps) for source in range(l...  50.1 us
    sub x8, matrix products, attend(): centred = (slopes - mean_slope) * (pulls - mean_pull)  35.7 us
    dot_general x4, matrix products, attend(): jnp.einsum('tgk,kd->tgd', coef_rounded, key_head, preferred_element_type=...  13.3 us
    sub x4, matrix products, attend(): exp_terms = jnp.exp(masked - row_max)  9.36 us
    dot_general x4, matrix products, attend(): jnp.einsum('tgd,kd->tgk', grad_head, value_head, preferred_element_type=j...  5.59 us
    psum x1, blocking collectives, per_device(): meta_gradient = lax.psum(new_solution, 'task') / lax.axis_size('task')  5 us
  transfers between devices with their start and end apart: 19, of which 2 were waited for; matrix products, arithmetic and copies ran while one was open for 3% of the time, Pallas kernels for 0%

commit v1 on v0

--- a/solution.py
+++ b/solution.py
@@ -110,7 +110,11 @@
     part_start = dev_index * part_size
     dir_part = lax.dynamic_slice_in_dim(dir_full, part_start, part_size, 0)
     sol_part = lax.dynamic_slice_in_dim(solution[0], part_start, part_size, 0)
-    complete_curvature_product = lax.psum(curvature_product_term, "ctx")
+    complete_curvature_product = curvature_product_term
+    for hop in (1, 2, 4, 8):
+        complete_curvature_product = complete_curvature_product + lax.ppermute(
+            complete_curvature_product, "ctx", [(dev, dev ^ hop) for dev in range(16)]
+        )
     curved = dir_full + complete_curvature_product / damp_val
     step_len = old_norm / jnp.sum(dir_full * curved)
     res_next = res_full - step_len * curved

time: 249 us -> 163 us (0.65)
  the two profiles are of different devices: /device:TPU:8 before, /device:TPU:0 now
where the time goes in v1:
time: 163 us; the launch traced here: 162 us
  matrix products  66.2 us (41%)
  starting transfers between devices  66 us (40%)
  waiting for transfers between devices  12.1 us (7%)
  other arithmetic  5.04 us (3%)
  blocking collectives  5 us (3%)
  between operations  4.73 us (3%)
  local copies, waits for them, and re-layouts  2.67 us (2%)
    ppermute x18, starting transfers between devices, passed_along(): lax.ppermute(value, axis, [(source, source + steps) for source in range(l...  50.8 us
    sub x8, matrix products, attend(): centred = (slopes - mean_slope) * (pulls - mean_pull)  35.7 us
    ppermute x4, starting transfers between devices, per_device(): lax.ppermute(complete_curvature_product, 'ctx', [(dev, dev ^ hop) for dev...  15.2 us
    dot_general x4, matrix products, attend(): jnp.einsum('tgk,kd->tgd', coef_rounded, key_head, preferred_element_type=...  13.3 us
    ppermute x4, waiting for transfers between devices, per_device(): lax.ppermute(complete_curvature_product, 'ctx', [(dev, dev ^ hop) for dev...  11.4 us
    sub x4, matrix products, attend(): exp_terms = jnp.exp(masked - row_max)  9.36 us
    dot_general x4, matrix products, attend(): jnp.einsum('tgd,kd->tgk', grad_head, value_head, preferred_element_type=j...  5.6 us
    psum x1, blocking collectives, per_device(): meta_gradient = lax.psum(new_solution, 'task') / lax.axis_size('task')  5 us
  transfers between devices with their start and end apart: 22, of which 5 were waited for; matrix products, arithmetic and copies ran while one was open for 4% of the time, Pallas kernels for 0%

profile of v1, /device:TPU:0, one launch (start us, length us, event | category | flops | bytes accessed | tf_op | source)
XLA Modules:
  0.0 161.8 jit_solution(15377277801215169079)
XLA Ops:
  0.7 6.0 %collective-permute-start = (s32[128]{0:T(128)}, s32[128]{0:T(128)S(1)}, u32[]{:S(2)}, u32[]{:S(2)}) collective-permute-start(s32[128]{0:T(128)} %bitcast.349), channel_id=1, source_target_pairs={{0,6},{1,7},{2,8},{3,9},{4,10},{5,11},{6,12},{7,13},{8,14},{9,15},... | collective-permute-start | bytes 1544 | tf_op jit(solution)/shard_map/ppermute | solution.py:16
  6.7 2.6 %collective-permute-start.1 = (s32[128]{0:T(128)}, s32[128]{0:T(128)S(1)}, u32[]{:S(2)}, u32[]{:S(2)}) collective-permute-start(s32[128]{0:T(128)} %bitcast.350), channel_id=1, source_target_pairs={{0,5},{1,6},{2,7},{3,8},{4,9},{5,10},{6,11},{7,12},{8,13},{9,14},{... | collective-permute-start | bytes 1544 | tf_op jit(solution)/shard_map/ppermute | solution.py:16
  9.4 3.5 %collective-permute-start.2 = (s32[128]{0:T(128)}, s32[128]{0:T(128)S(1)}, u32[]{:S(2)}, u32[]{:S(2)}) collective-permute-start(s32[128]{0:T(128)} %bitcast.351), channel_id=1, source_target_pairs={{0,4},{1,5},{2,6},{3,7},{4,8},{5,9},{6,10},{7,11},{8,12},{9,13},{1... | collective-permute-start | bytes 1544 | tf_op jit(solution)/shard_map/ppermute | solution.py:16
  12.9 2.8 %collective-permute-start.3 = (s32[128]{0:T(128)}, s32[128]{0:T(128)S(1)}, u32[]{:S(2)}, u32[]{:S(2)}) collective-permute-start(s32[128]{0:T(128)} %bitcast.352), channel_id=1, source_target_pairs={{0,3},{1,4},{2,5},{3,6},{4,7},{5,8},{6,9},{7,10},{8,11},{9,12},{10... | collective-permute-start | bytes 1544 | tf_op jit(solution)/shard_map/ppermute | solution.py:16
  15.6 2.3 %collective-permute-start.4 = (s32[128]{0:T(128)}, s32[128]{0:T(128)S(1)}, u32[]{:S(2)}, u32[]{:S(2)}) collective-permute-start(s32[128]{0:T(128)} %bitcast.353), channel_id=1, source_target_pairs={{0,2},{1,3},{2,4},{3,5},{4,6},{5,7},{6,8},{7,9},{8,10},{9,11},{10,... | collective-permute-start | bytes 1544 | tf_op jit(solution)/shard_map/ppermute | solution.py:16
  17.9 1.4 fusion.12
  20.9 0.9 reduce.3
  23.3 1.7 %collective-permute-start.5 = (s32[128]{0:T(128)S(1)}, s32[128]{0:T(128)S(1)}, u32[]{:S(2)}, u32[]{:S(2)}) collective-permute-start(s32[128]{0:T(128)S(1)} %bitcast.354), channel_id=1, source_target_pairs={{0,1},{1,2},{2,3},{3,4},{4,5},{5,6},{6,7},{7,8},{8,9},{9,10},{10,1... | collective-permute-start | bytes 1544 | tf_op jit(solution)/shard_map/ppermute | solution.py:16
  25.1 2.7 %collective-permute-start.6 = (bf16[128,512]{1,0:T(8,128)(2,1)S(1)}, bf16[128,512]{1,0:T(8,128)(2,1)S(1)}, u32[]{:S(2)}, u32[]{:S(2)}) collective-permute-start(bf16[128,512]{1,0:T(8,128)(2,1)S(1)} %bitcast.333), channel_id=1, source_target_pairs={{0,6},{1,7},{2,8},{3,9},{4,10},{5,11},{6,12},{7,13},{8,14},{9,15},... | collective-permute-start | bytes 393224 | tf_op jit(solution)/shard_map/ppermute | solution.py:16
  27.8 1.6 collective-permute-start.7
  29.4 1.3 collective-permute-start.8
  30.8 2.9 %collective-permute-start.9 = (bf16[128,512]{1,0:T(8,128)(2,1)S(1)}, bf16[128,512]{1,0:T(8,128)(2,1)S(1)}, u32[]{:S(2)}, u32[]{:S(2)}) collective-permute-start(bf16[128,512]{1,0:T(8,128)(2,1)S(1)} %bitcast.336), channel_id=1, source_target_pairs={{0,3},{1,4},{2,5},{3,6},{4,7},{5,8},{6,9},{7,10},{8,11},{9,12},{10... | collective-permute-start | bytes 393224 | tf_op jit(solution)/shard_map/ppermute | solution.py:16
  33.7 3.0 %collective-permute-start.10 = (bf16[128,512]{1,0:T(8,128)(2,1)S(1)}, bf16[128,512]{1,0:T(8,128)(2,1)S(1)}, u32[]{:S(2)}, u32[]{:S(2)}) collective-permute-start(bf16[128,512]{1,0:T(8,128)(2,1)S(1)} %bitcast.337), channel_id=1, source_target_pairs={{0,2},{1,3},{2,4},{3,5},{4,6},{5,7},{6,8},{7,9},{8,10},{9,11},{10,... | collective-permute-start | bytes 393224 | tf_op jit(solution)/shard_map/ppermute | solution.py:16
  37.0 1.4 collective-permute-start.11
  38.5 2.2 %collective-permute-start.12 = (bf16[128,512]{1,0:T(8,128)(2,1)S(1)}, bf16[128,512]{1,0:T(8,128)(2,1)S(1)}, u32[]{:S(2)}, u32[]{:S(2)}) collective-permute-start(bf16[128,512]{1,0:T(8,128)(2,1)S(1)} %bitcast.339), channel_id=1, source_target_pairs={{0,6},{1,7},{2,8},{3,9},{4,10},{5,11},{6,12},{7,13},{8,14},{9,15},... | collective-permute-start | bytes 393224 | tf_op jit(solution)/shard_map/ppermute | solution.py:16
  40.7 5.4 %collective-permute-start.13 = (bf16[128,512]{1,0:T(8,128)(2,1)S(1)}, bf16[128,512]{1,0:T(8,128)(2,1)S(1)}, u32[]{:S(2)}, u32[]{:S(2)}) collective-permute-start(bf16[128,512]{1,0:T(8,128)(2,1)S(1)} %bitcast.340), channel_id=1, source_target_pairs={{0,5},{1,6},{2,7},{3,8},{4,9},{5,10},{6,11},{7,12},{8,13},{9,14},{... | collective-permute-start | bytes 393224 | tf_op jit(solution)/shard_map/ppermute | solution.py:16
  46.2 1.3 collective-permute-start.14
  47.5 1.9 %collective-permute-start.15 = (bf16[128,512]{1,0:T(8,128)(2,1)S(1)}, bf16[128,512]{1,0:T(8,128)(2,1)S(1)}, u32[]{:S(2)}, u32[]{:S(2)}) collective-permute-start(bf16[128,512]{1,0:T(8,128)(2,1)S(1)} %bitcast.342), channel_id=1, source_target_pairs={{0,3},{1,4},{2,5},{3,6},{4,7},{5,8},{6,9},{7,10},{8,11},{9,12},{10... | collective-permute-start | bytes 393224 | tf_op jit(solution)/shard_map/ppermute | solution.py:16
  49.5 4.6 %collective-permute-start.16 = (bf16[128,512]{1,0:T(8,128)(2,1)S(1)}, bf16[128,512]{1,0:T(8,128)(2,1)S(1)}, u32[]{:S(2)}, u32[]{:S(2)}) collective-permute-start(bf16[128,512]{1,0:T(8,128)(2,1)S(1)} %bitcast.343), channel_id=1, source_target_pairs={{0,2},{1,3},{2,4},{3,5},{4,6},{5,7},{6,8},{7,9},{8,10},{9,11},{10,... | collective-permute-start | bytes 393224 | tf_op jit(solution)/shard_map/ppermute | solution.py:16
  54.1 3.5 %collective-permute-start.17 = (bf16[128,512]{1,0:T(8,128)(2,1)S(1)}, bf16[128,512]{1,0:T(8,128)(2,1)S(1)}, u32[]{:S(2)}, u32[]{:S(2)}) collective-permute-start(bf16[128,512]{1,0:T(8,128)(2,1)S(1)} %bitcast.344), channel_id=1, source_target_pairs={{0,1},{1,2},{2,3},{3,4},{4,5},{5,6},{6,7},{7,8},{8,9},{9,10},{10,1... | collective-permute-start | bytes 393224 | tf_op jit(solution)/shard_map/ppermute | solution.py:16
  58.5 3.1 %fusion.228 = (f32[128,4]{0,1:T(4,128)S(1)}, f32[128,4,896]{2,0,1:T(8,128)}) fusion(pred[128,896]{1,0:T(8,128)(4,1)S(1)} %compare_and_fusion, bf16[16,4,8,128]{3,2,1,0:T(8,128)(2,1)S(1)} %copy-done.11, bf16[896,512]{1,0:T(8,128)(2,1)} %copy-done.15), kind=kOutput, calls=%fused_computation.226 | convolution fusion | flops 119276416 | bytes 2312192 | tf_op jit(solution)/shard_map/sub | solution.py:44
  61.6 2.1 %fusion.221 = (f32[128,4]{0,1:T(4,128)S(1)}, f32[128,4,896]{2,0,1:T(8,128)}) fusion(pred[128,896]{1,0:T(8,128)(4,1)S(1)} %compare_and_fusion, bf16[16,4,8,128]{3,2,1,0:T(8,128)(2,1)S(1)} %get-tuple-element.15, bf16[896,512]{1,0:T(8,128)(2,1)S(1)} %copy-done.16), kind=kOutput, calls=%fused_computation.225 | convolution fusion | flops 119276416 | bytes 2312192 | tf_op jit(solution)/shard_map/sub | solution.py:44
  63.7 1.7 %fusion.75 = f32[896,128,4]{0,1,2:T(8,128)} fusion(bf16[128,4,128]{0,2,1:T(8,128)(2,1)S(1)} %bitcast.331, bf16[896,512]{1,0:T(8,128)(2,1)S(1)} %constant_dynamic-update-slice_fusion.8), kind=kOutput, calls=%fused_computation.114 | convolution fusion | flops 117440512 | bytes 2195456 | tf_op jit(solution)/shard_map/tgd,kd->tgk/dot_general | solution.py:40
  65.4 1.8 %fusion.74 = f32[896,128,4]{0,1,2:T(8,128)} fusion(bf16[128,4,128]{0,2,1:T(8,128)(2,1)S(1)} %bitcast.329, bf16[896,512]{1,0:T(8,128)(2,1)S(1)} %constant_dynamic-update-slice_fusion.8), kind=kOutput, calls=%fused_computation.111 | convolution fusion | flops 117440512 | bytes 2195456 | tf_op jit(solution)/shard_map/tgd,kd->tgk/dot_general | solution.py:40
  67.2 2.1 %fusion.214 = (f32[128,4]{0,1:T(4,128)S(1)}, f32[128,4,896]{2,0,1:T(8,128)}) fusion(pred[128,896]{1,0:T(8,128)(4,1)S(1)} %compare_and_fusion, bf16[16,4,8,128]{3,2,1,0:T(8,128)(2,1)S(1)} %get-tuple-element.14, bf16[896,512]{1,0:T(8,128)(2,1)S(1)} %copy-done.16), kind=kOutput, calls=%fused_computation.224 | convolution fusion | flops 119276416 | bytes 2312192 | tf_op jit(solution)/shard_map/sub | solution.py:44
  69.2 1.7 %fusion.73 = f32[896,128,4]{0,1,2:T(8,128)} fusion(bf16[128,4,128]{0,2,1:T(8,128)(2,1)S(1)} %bitcast.327, bf16[896,512]{1,0:T(8,128)(2,1)S(1)} %constant_dynamic-update-slice_fusion.8), kind=kOutput, calls=%fused_computation.108 | convolution fusion | flops 117440512 | bytes 2195456 | tf_op jit(solution)/shard_map/tgd,kd->tgk/dot_general | solution.py:40
  70.9 2.1 %fusion.207 = (f32[128,4]{0,1:T(4,128)S(1)}, f32[128,4,896]{2,0,1:T(8,128)}) fusion(pred[128,896]{1,0:T(8,128)(4,1)S(1)} %compare_and_fusion, bf16[16,4,8,128]{3,2,1,0:T(8,128)(2,1)S(1)} %get-tuple-element.13, bf16[896,512]{1,0:T(8,128)(2,1)S(1)} %copy-done.16), kind=kOutput, calls=%fused_computation.223 | convolution fusion | flops 119276416 | bytes 2312192 | tf_op jit(solution)/shard_map/sub | solution.py:44
  73.5 3.4 %fusion.9 = f32[128,4,896]{2,0,1:T(8,128)} fusion(bf16[128,4,128]{0,2,1:T(8,128)(2,1)S(1)} %bitcast.332, bf16[896,512]{1,0:T(8,128)(2,1)S(1)} %constant_dynamic-update-slice_fusion.8, f32[128,4,896]{2,0,1:T(8,128)} %get-tuple-element.35, f32[128,4]{0,1:T(4,128)S(1)} %get-tuple-element.34), kind=kOutput, calls=%fused_computation.9 | convolution fusion | flops 118359424 | bytes 4032512 | tf_op jit(solution)/shard_map/sub | solution.py:48
  76.8 5.7 %multiply_reduce_fusion.6 = (f32[128,4]{0,1:T(4,128)S(1)}, f32[128,4,896]{2,0,1:T(8,128)}) fusion(f32[128,4,896]{2,0,1:T(8,128)} %get-tuple-element.35, f32[128,4]{0,1:T(4,128)S(1)} %get-tuple-element.34, f32[128,4,896]{2,0,1:T(8,128)} %fusion.9, f32[896,128,4]{0,1,2:T(8,128)} %fusion.75, bf16[16,4,8,128]{3,2,1,0:T(8,128)(2,1)} %get-tuple-element.8, ...), kind=kOutput, calls=%fused_computation.46 | convolution fusion | flops 239469440 | bytes 9902080 | tf_op jit(solution)/shard_map/sub | solution.py:48
  82.5 3.8 %fusion.37 = bf16[128,4,128]{0,2,1:T(8,128)(2,1)} fusion(f32[128,4,896]{2,0,1:T(8,128)} %get-tuple-element.37, f32[128,4]{0,1:T(4,128)S(1)} %get-tuple-element.36, bf16[896,512]{1,0:T(8,128)(2,1)} %copy-done.15, f32[128,4]{0,1:T(4,128)S(1)} %get-tuple-element.34, pred[128,896]{1,0:T(8,128)(4,1)} %copy-done.13, bf16[16,4,8,128]{3,2,1,0:T(8,128)(2,1)} %get-tuple-element.12), kind=kOutput, calls=%fused_computation.63 | convolution fusion | flops 238224768 | bytes 2674688 | tf_op jit(solution)/shard_map/tgk,kd->tgd/dot_general | solution.py:52
  86.3 3.4 %fusion.6 = f32[128,4,896]{2,0,1:T(8,128)} fusion(bf16[128,4,128]{0,2,1:T(8,128)(2,1)S(1)} %bitcast.330, bf16[896,512]{1,0:T(8,128)(2,1)S(1)} %constant_dynamic-update-slice_fusion.8, f32[128,4,896]{2,0,1:T(8,128)} %get-tuple-element.31, f32[128,4]{0,1:T(4,128)S(1)} %get-tuple-element.30), kind=kOutput, calls=%fused_computation.6 | convolution fusion | flops 118359424 | bytes 4032512 | tf_op jit(solution)/shard_map/sub | solution.py:48
  89.7 5.6 %multiply_reduce_fusion.4 = (f32[128,4]{0,1:T(4,128)S(1)}, f32[128,4,896]{2,0,1:T(8,128)}) fusion(f32[128,4,896]{2,0,1:T(8,128)} %get-tuple-element.31, f32[128,4]{0,1:T(4,128)S(1)} %get-tuple-element.30, f32[128,4,896]{2,0,1:T(8,128)} %fusion.6, f32[896,128,4]{0,1,2:T(8,128)} %fusion.74, bf16[16,4,8,128]{3,2,1,0:T(8,128)(2,1)S(1)} %copy-done.12, ...), kind=kOutput, calls=%fused_computation.40 | convolution fusion | flops 239469440 | bytes 9902080 | tf_op jit(solution)/shard_map/sub | solution.py:48
  95.3 3.2 %fusion.38 = bf16[128,4,128]{0,2,1:T(8,128)(2,1)S(1)} fusion(f32[128,4,896]{2,0,1:T(8,128)} %get-tuple-element.33, f32[128,4]{0,1:T(4,128)S(1)} %get-tuple-element.32, bf16[896,512]{1,0:T(8,128)(2,1)} %copy-done.15, f32[128,4]{0,1:T(4,128)S(1)} %get-tuple-element.30, pred[128,896]{1,0:T(8,128)(4,1)} %copy-done.13, bf16[16,4,8,128]{3,2,1,0:T(8,128)(2,1)} %copy-done.9), kind=kOutput, calls=%fused_computation.64 | convolution fusion | flops 238224768 | bytes 2674688 | tf_op jit(solution)/shard_map/tgk,kd->tgd/dot_general | solution.py:52
  98.5 3.4 %fusion.3 = f32[128,4,896]{2,0,1:T(8,128)} fusion(bf16[128,4,128]{0,2,1:T(8,128)(2,1)S(1)} %bitcast.328, bf16[896,512]{1,0:T(8,128)(2,1)S(1)} %constant_dynamic-update-slice_fusion.8, f32[128,4,896]{2,0,1:T(8,128)} %get-tuple-element.27, f32[128,4]{0,1:T(4,128)S(1)} %get-tuple-element.26), kind=kOutput, calls=%fused_computation.3 | convolution fusion | flops 118359424 | bytes 4032512 | tf_op jit(solution)/shard_map/sub | solution.py:48
  101.9 5.8 %multiply_reduce_fusion.2 = (f32[128,4]{0,1:T(4,128)S(1)}, f32[128,4,896]{2,0,1:T(8,128)}) fusion(f32[128,4,896]{2,0,1:T(8,128)} %get-tuple-element.27, f32[128,4]{0,1:T(4,128)S(1)} %get-tuple-element.26, f32[128,4,896]{2,0,1:T(8,128)} %fusion.3, f32[896,128,4]{0,1,2:T(8,128)} %fusion.73, bf16[16,4,8,128]{3,2,1,0:T(8,128)(2,1)S(1)} %copy-done.10, ...), kind=kOutput, calls=%fused_computation.34 | convolution fusion | flops 239469440 | bytes 9902080 | tf_op jit(solution)/shard_map/sub | solution.py:48
  107.7 3.2 %fusion.39 = bf16[128,4,128]{0,2,1:T(8,128)(2,1)S(1)} fusion(f32[128,4,896]{2,0,1:T(8,128)} %get-tuple-element.29, f32[128,4]{0,1:T(4,128)S(1)} %get-tuple-element.28, bf16[896,512]{1,0:T(8,128)(2,1)} %copy-done.15, f32[128,4]{0,1:T(4,128)S(1)} %get-tuple-element.26, pred[128,896]{1,0:T(8,128)(4,1)} %copy-done.13, bf16[16,4,8,128]{3,2,1,0:T(8,128)(2,1)} %copy-done.7), kind=kOutput, calls=%fused_computation.65 | convolution fusion | flops 238224768 | bytes 2674688 | tf_op jit(solution)/shard_map/tgk,kd->tgd/dot_general | solution.py:52
  110.9 3.3 %fusion = f32[128,4,896]{2,0,1:T(8,128)} fusion(bf16[128,4,128]{0,2,1:T(8,128)(2,1)S(1)} %bitcast.326, bf16[896,512]{1,0:T(8,128)(2,1)S(1)} %constant_dynamic-update-slice_fusion.8, f32[128,4,896]{2,0,1:T(8,128)} %get-tuple-element.23, f32[128,4]{0,1:T(4,128)S(1)} %get-tuple-element.22), kind=kOutput, calls=%fused_computation | convolution fusion | flops 118359424 | bytes 4032512 | tf_op jit(solution)/shard_map/sub | solution.py:48
  114.3 5.1 %multiply_reduce_fusion = (f32[128,4]{0,1:T(4,128)S(1)}, f32[128,4,896]{2,0,1:T(8,128)}) fusion(f32[128,4,896]{2,0,1:T(8,128)} %get-tuple-element.23, f32[128,4]{0,1:T(4,128)S(1)} %get-tuple-element.22, f32[128,4,896]{2,0,1:T(8,128)} %fusion, f32[896,128,4]{0,1,2:T(8,128)S(1)} %fusion.72, bf16[16,4,8,128]{3,2,1,0:T(8,128)(2,1)S(1)} %copy-done.8, ...), kind=kOutput, calls=%fused_computation.28 | convolution fusion | flops 239469440 | bytes 9902080 | tf_op jit(solution)/shard_map/sub | solution.py:48
  119.4 3.2 %fusion.40 = bf16[128,4,128]{0,2,1:T(8,128)(2,1)S(1)} fusion(f32[128,4,896]{2,0,1:T(8,128)} %get-tuple-element.25, f32[128,4]{0,1:T(4,128)S(1)} %get-tuple-element.24, bf16[896,512]{1,0:T(8,128)(2,1)S(1)} %copy-done.17, f32[128,4]{0,1:T(4,128)S(1)} %get-tuple-element.22, pred[128,896]{1,0:T(8,128)(4,1)} %copy-done.13, bf16[16,4,8,128]{3,2,1,0:T(8,128)(2,1)} %copy-done.6), kind=kOutput, calls=%fused_computation.66 | convolution fusion | flops 238224768 | bytes 2674688 | tf_op jit(solution)/shard_map/tgk,kd->tgd/dot_general | solution.py:52
  122.8 1.1 collective-permute-start.18
  123.9 1.0 collective-permute-done.18
  124.9 3.5 %collective-permute-start.19 = (f32[32768]{0:T(1024)S(1)}, f32[32768]{0:T(1024)S(1)}, u32[]{:S(2)}, u32[]{:S(2)}) collective-permute-start(f32[32768]{0:T(1024)S(1)} %add.65), channel_id=1, source_target_pairs={{0,2},{1,3},{2,0},{3,1},{4,6},{5,7},{6,4},{7,5},{8,10},{9,11},{10,... | collective-permute-start | bytes 393224 | tf_op jit(solution)/shard_map/ppermute | solution.py:115
  128.5 4.0 %collective-permute-done.19 = f32[32768]{0:T(1024)S(1)} collective-permute-done((f32[32768]{0:T(1024)S(1)}, f32[32768]{0:T(1024)S(1)}, u32[]{:S(2)}, u32[]{:S(2)}) %collective-permute-start.19) | collective-permute-done | bytes 131104 | tf_op jit(solution)/shard_map/ppermute | solution.py:115
  132.5 5.5 %collective-permute-start.20 = (f32[32768]{0:T(1024)S(1)}, f32[32768]{0:T(1024)S(1)}, u32[]{:S(2)}, u32[]{:S(2)}) collective-permute-start(f32[32768]{0:T(1024)S(1)} %add.66), channel_id=1, source_target_pairs={{0,4},{1,5},{2,6},{3,7},{4,0},{5,1},{6,2},{7,3},{8,12},{9,13},{10,... | collective-permute-start | bytes 393224 | tf_op jit(solution)/shard_map/ppermute | solution.py:115
  138.1 3.4 %collective-permute-done.20 = f32[32768]{0:T(1024)S(1)} collective-permute-done((f32[32768]{0:T(1024)S(1)}, f32[32768]{0:T(1024)S(1)}, u32[]{:S(2)}, u32[]{:S(2)}) %collective-permute-start.20) | collective-permute-done | bytes 131104 | tf_op jit(solution)/shard_map/ppermute | solution.py:115
  141.5 5.0 %collective-permute-start.21 = (f32[32768]{0:T(1024)S(1)}, f32[32768]{0:T(1024)S(1)}, u32[]{:S(2)}, u32[]{:S(2)}) collective-permute-start(f32[32768]{0:T(1024)S(1)} %add.67), channel_id=1, source_target_pairs={{0,8},{1,9},{2,10},{3,11},{4,12},{5,13},{6,14},{7,15},{8,0},{9,1},... | collective-permute-start | bytes 393224 | tf_op jit(solution)/shard_map/ppermute | solution.py:115
  147.9 3.0 %collective-permute-done.21 = f32[32768]{0:T(1024)S(1)} collective-permute-done((f32[32768]{0:T(1024)S(1)}, f32[32768]{0:T(1024)S(1)}, u32[]{:S(2)}, u32[]{:S(2)}) %collective-permute-start.21) | collective-permute-done | bytes 131104 | tf_op jit(solution)/shard_map/ppermute | solution.py:115
  155.5 5.0 %psum.7 = f32[2048]{0:T(1024)S(1)} all-reduce(f32[2048]{0:T(1024)S(1)} %bitcast.345), channel_id=1, replica_groups=mesh['task'=2,'ctx'=16] {'task'}, use_global_device_ids=true, to_apply=%region_23.24 | all-reduce | flops 2048 | bytes 16384 | tf_op jit(solution)/shard_map/psum | solution.py:125
  (105 shorter events, 8.7 us)
Async XLA Ops:
  0.6 17.3 %copy-start = (bf16[1,16,2048]{2,1,0:T(8,128)(2,1)S(1)}, bf16[1,16,2048]{2,1,0:T(8,128)(2,1)}, u32[]{:S(2)}) copy-start(bf16[1,16,2048]{2,1,0:T(8,128)(2,1)} %param.13) | copy-start | bytes 196612
  0.6 19.4 %copy-start.2 = (bf16[1,128,2048]{2,1,0:T(8,128)(2,1)S(1)}, bf16[1,128,2048]{2,1,0:T(8,128)(2,1)}, u32[]{:S(2)}) copy-start(bf16[1,128,2048]{2,1,0:T(8,128)(2,1)} %param.16) | copy-start | bytes 1572868
  0.7 22.7 %collective-permute-start = (s32[128]{0:T(128)}, s32[128]{0:T(128)S(1)}, u32[]{:S(2)}, u32[]{:S(2)}) collective-permute-start(s32[128]{0:T(128)} %bitcast.349), channel_id=1, source_target_pairs={{0,6},{1,7},{2,8},{3,9},{4,10},{5,11},{6,12},{7,13},{8,14},{9,15},... | collective-permute-start | bytes 1544 | tf_op jit(solution)/shard_map/ppermute | solution.py:16
  6.7 18.3 %collective-permute-start.1 = (s32[128]{0:T(128)}, s32[128]{0:T(128)S(1)}, u32[]{:S(2)}, u32[]{:S(2)}) collective-permute-start(s32[128]{0:T(128)} %bitcast.350), channel_id=1, source_target_pairs={{0,5},{1,6},{2,7},{3,8},{4,9},{5,10},{6,11},{7,12},{8,13},{9,14},{... | collective-permute-start | bytes 1544 | tf_op jit(solution)/shard_map/ppermute | solution.py:16
  9.4 18.5 %collective-permute-start.2 = (s32[128]{0:T(128)}, s32[128]{0:T(128)S(1)}, u32[]{:S(2)}, u32[]{:S(2)}) collective-permute-start(s32[128]{0:T(128)} %bitcast.351), channel_id=1, source_target_pairs={{0,4},{1,5},{2,6},{3,7},{4,8},{5,9},{6,10},{7,11},{8,12},{9,13},{1... | collective-permute-start | bytes 1544 | tf_op jit(solution)/shard_map/ppermute | solution.py:16
  12.9 16.6 %collective-permute-start.3 = (s32[128]{0:T(128)}, s32[128]{0:T(128)S(1)}, u32[]{:S(2)}, u32[]{:S(2)}) collective-permute-start(s32[128]{0:T(128)} %bitcast.352), channel_id=1, source_target_pairs={{0,3},{1,4},{2,5},{3,6},{4,7},{5,8},{6,9},{7,10},{8,11},{9,12},{10... | collective-permute-start | bytes 1544 | tf_op jit(solution)/shard_map/ppermute | solution.py:16
  15.6 15.1 %collective-permute-start.4 = (s32[128]{0:T(128)}, s32[128]{0:T(128)S(1)}, u32[]{:S(2)}, u32[]{:S(2)}) collective-permute-start(s32[128]{0:T(128)} %bitcast.353), channel_id=1, source_target_pairs={{0,2},{1,3},{2,4},{3,5},{4,6},{5,7},{6,8},{7,9},{8,10},{9,11},{10,... | collective-permute-start | bytes 1544 | tf_op jit(solution)/shard_map/ppermute | solution.py:16
  19.3 1.6 copy-start.1
  19.3 2.6 %copy-start.18 = (bf16[1,128,16]{1,2,0:T(8,128)(2,1)S(1)}, bf16[1,128,16]{1,2,0:T(8,128)(2,1)}, u32[]{:S(2)}) copy-start(bf16[1,128,16]{1,2,0:T(8,128)(2,1)} %param.12) | copy-start | bytes 12292
  20.0 41.6 %copy-start.9 = (bf16[16,4,8,128]{3,2,1,0:T(8,128)(2,1)}, bf16[16,4,8,128]{3,2,1,0:T(8,128)(2,1)S(1)}, u32[]{:S(2)}) copy-start(bf16[16,4,8,128]{3,2,1,0:T(8,128)(2,1)S(1)} %get-tuple-element.15) | copy-start | bytes 393220
  20.0 47.1 %copy-start.7 = (bf16[16,4,8,128]{3,2,1,0:T(8,128)(2,1)}, bf16[16,4,8,128]{3,2,1,0:T(8,128)(2,1)S(1)}, u32[]{:S(2)}) copy-start(bf16[16,4,8,128]{3,2,1,0:T(8,128)(2,1)S(1)} %get-tuple-element.14) | copy-start | bytes 393220
  20.0 50.9 %copy-start.6 = (bf16[16,4,8,128]{3,2,1,0:T(8,128)(2,1)}, bf16[16,4,8,128]{3,2,1,0:T(8,128)(2,1)S(1)}, u32[]{:S(2)}) copy-start(bf16[16,4,8,128]{3,2,1,0:T(8,128)(2,1)S(1)} %get-tuple-element.13) | copy-start | bytes 393220
  20.3 3.0 %copy-start.19 = (s32[1,128]{1,0:T(1,128)S(1)}, s32[1,128]{1,0:T(1,128)}, u32[]{:S(2)}) copy-start(s32[1,128]{1,0:T(1,128)} %param.17) | copy-start | bytes 1540
  20.3 4.7 %copy-start.4 = (bf16[1,128,512]{2,1,0:T(8,128)(2,1)S(1)}, bf16[1,128,512]{2,1,0:T(8,128)(2,1)}, u32[]{:S(2)}) copy-start(bf16[1,128,512]{2,1,0:T(8,128)(2,1)} %param.14) | copy-start | bytes 393220
  20.3 18.1 %copy-start.5 = (bf16[1,128,512]{2,1,0:T(8,128)(2,1)S(1)}, bf16[1,128,512]{2,1,0:T(8,128)(2,1)}, u32[]{:S(2)}) copy-start(bf16[1,128,512]{2,1,0:T(8,128)(2,1)} %param.15) | copy-start | bytes 393220
  23.3 10.3 %collective-permute-start.5 = (s32[128]{0:T(128)S(1)}, s32[128]{0:T(128)S(1)}, u32[]{:S(2)}, u32[]{:S(2)}) collective-permute-start(s32[128]{0:T(128)S(1)} %bitcast.354), channel_id=1, source_target_pairs={{0,1},{1,2},{2,3},{3,4},{4,5},{5,6},{6,7},{7,8},{8,9},{9,10},{10,1... | collective-permute-start | bytes 1544 | tf_op jit(solution)/shard_map/ppermute | solution.py:16
  25.1 11.9 %collective-permute-start.6 = (bf16[128,512]{1,0:T(8,128)(2,1)S(1)}, bf16[128,512]{1,0:T(8,128)(2,1)S(1)}, u32[]{:S(2)}, u32[]{:S(2)}) collective-permute-start(bf16[128,512]{1,0:T(8,128)(2,1)S(1)} %bitcast.333), channel_id=1, source_target_pairs={{0,6},{1,7},{2,8},{3,9},{4,10},{5,11},{6,12},{7,13},{8,14},{9,15},... | collective-permute-start | bytes 393224 | tf_op jit(solution)/shard_map/ppermute | solution.py:16
  27.8 10.6 %collective-permute-start.7 = (bf16[128,512]{1,0:T(8,128)(2,1)S(1)}, bf16[128,512]{1,0:T(8,128)(2,1)S(1)}, u32[]{:S(2)}, u32[]{:S(2)}) collective-permute-start(bf16[128,512]{1,0:T(8,128)(2,1)S(1)} %bitcast.334), channel_id=1, source_target_pairs={{0,5},{1,6},{2,7},{3,8},{4,9},{5,10},{6,11},{7,12},{8,13},{9,14},{... | collective-permute-start | bytes 393224 | tf_op jit(solution)/shard_map/ppermute | solution.py:16
  29.4 11.3 %collective-permute-start.8 = (bf16[128,512]{1,0:T(8,128)(2,1)S(1)}, bf16[128,512]{1,0:T(8,128)(2,1)S(1)}, u32[]{:S(2)}, u32[]{:S(2)}) collective-permute-start(bf16[128,512]{1,0:T(8,128)(2,1)S(1)} %bitcast.335), channel_id=1, source_target_pairs={{0,4},{1,5},{2,6},{3,7},{4,8},{5,9},{6,10},{7,11},{8,12},{9,13},{1... | collective-permute-start | bytes 393224 | tf_op jit(solution)/shard_map/ppermute | solution.py:16
  30.8 15.4 %collective-permute-start.9 = (bf16[128,512]{1,0:T(8,128)(2,1)S(1)}, bf16[128,512]{1,0:T(8,128)(2,1)S(1)}, u32[]{:S(2)}, u32[]{:S(2)}) collective-permute-start(bf16[128,512]{1,0:T(8,128)(2,1)S(1)} %bitcast.336), channel_id=1, source_target_pairs={{0,3},{1,4},{2,5},{3,6},{4,7},{5,8},{6,9},{7,10},{8,11},{9,12},{10... | collective-permute-start | bytes 393224 | tf_op jit(solution)/shard_map/ppermute | solution.py:16
  33.7 13.8 %collective-permute-start.10 = (bf16[128,512]{1,0:T(8,128)(2,1)S(1)}, bf16[128,512]{1,0:T(8,128)(2,1)S(1)}, u32[]{:S(2)}, u32[]{:S(2)}) collective-permute-start(bf16[128,512]{1,0:T(8,128)(2,1)S(1)} %bitcast.337), channel_id=1, source_target_pairs={{0,2},{1,3},{2,4},{3,5},{4,6},{5,7},{6,8},{7,9},{8,10},{9,11},{10,... | collective-permute-start | bytes 393224 | tf_op jit(solution)/shard_map/ppermute | solution.py:16
  37.0 34.0 %copy-start.13 = (pred[128,896]{1,0:T(8,128)(4,1)}, pred[128,896]{1,0:T(8,128)(4,1)S(1)}, u32[]{:S(2)}) copy-start(pred[128,896]{1,0:T(8,128)(4,1)S(1)} %compare_and_fusion) | copy-start | bytes 344068
  37.0 21.5 %copy-start.11 = (bf16[16,4,8,128]{3,2,1,0:T(8,128)(2,1)S(1)}, bf16[16,4,8,128]{3,2,1,0:T(8,128)(2,1)}, u32[]{:S(2)}) copy-start(bf16[16,4,8,128]{3,2,1,0:T(8,128)(2,1)} %get-tuple-element.12) | copy-start | bytes 393220
  37.0 12.5 %collective-permute-start.11 = (bf16[128,512]{1,0:T(8,128)(2,1)S(1)}, bf16[128,512]{1,0:T(8,128)(2,1)S(1)}, u32[]{:S(2)}, u32[]{:S(2)}) collective-permute-start(bf16[128,512]{1,0:T(8,128)(2,1)S(1)} %bitcast.338), channel_id=1, source_target_pairs={{0,1},{1,2},{2,3},{3,4},{4,5},{5,6},{6,7},{7,8},{8,9},{9,10},{10,1... | collective-permute-start | bytes 393224 | tf_op jit(solution)/shard_map/ppermute | solution.py:16
  38.5 15.7 %collective-permute-start.12 = (bf16[128,512]{1,0:T(8,128)(2,1)S(1)}, bf16[128,512]{1,0:T(8,128)(2,1)S(1)}, u32[]{:S(2)}, u32[]{:S(2)}) collective-permute-start(bf16[128,512]{1,0:T(8,128)(2,1)S(1)} %bitcast.339), channel_id=1, source_target_pairs={{0,6},{1,7},{2,8},{3,9},{4,10},{5,11},{6,12},{7,13},{8,14},{9,15},... | collective-permute-start | bytes 393224 | tf_op jit(solution)/shard_map/ppermute | solution.py:16
  40.7 17.0 %collective-permute-start.13 = (bf16[128,512]{1,0:T(8,128)(2,1)S(1)}, bf16[128,512]{1,0:T(8,128)(2,1)S(1)}, u32[]{:S(2)}, u32[]{:S(2)}) collective-permute-start(bf16[128,512]{1,0:T(8,128)(2,1)S(1)} %bitcast.340), channel_id=1, source_target_pairs={{0,5},{1,6},{2,7},{3,8},{4,9},{5,10},{6,11},{7,12},{8,13},{9,14},{... | collective-permute-start | bytes 393224 | tf_op jit(solution)/shard_map/ppermute | solution.py:16
  46.2 11.5 %collective-permute-start.14 = (bf16[128,512]{1,0:T(8,128)(2,1)S(1)}, bf16[128,512]{1,0:T(8,128)(2,1)S(1)}, u32[]{:S(2)}, u32[]{:S(2)}) collective-permute-start(bf16[128,512]{1,0:T(8,128)(2,1)S(1)} %bitcast.341), channel_id=1, source_target_pairs={{0,4},{1,5},{2,6},{3,7},{4,8},{5,9},{6,10},{7,11},{8,12},{9,13},{1... | collective-permute-start | bytes 393224 | tf_op jit(solution)/shard_map/ppermute | solution.py:16
  47.5 10.2 %collective-permute-start.15 = (bf16[128,512]{1,0:T(8,128)(2,1)S(1)}, bf16[128,512]{1,0:T(8,128)(2,1)S(1)}, u32[]{:S(2)}, u32[]{:S(2)}) collective-permute-start(bf16[128,512]{1,0:T(8,128)(2,1)S(1)} %bitcast.342), channel_id=1, source_target_pairs={{0,3},{1,4},{2,5},{3,6},{4,7},{5,8},{6,9},{7,10},{8,11},{9,12},{10... | collective-permute-start | bytes 393224 | tf_op jit(solution)/shard_map/ppermute | solution.py:16
  49.5 8.3 %collective-permute-start.16 = (bf16[128,512]{1,0:T(8,128)(2,1)S(1)}, bf16[128,512]{1,0:T(8,128)(2,1)S(1)}, u32[]{:S(2)}, u32[]{:S(2)}) collective-permute-start(bf16[128,512]{1,0:T(8,128)(2,1)S(1)} %bitcast.343), channel_id=1, source_target_pairs={{0,2},{1,3},{2,4},{3,5},{4,6},{5,7},{6,8},{7,9},{8,10},{9,11},{10,... | collective-permute-start | bytes 393224 | tf_op jit(solution)/shard_map/ppermute | solution.py:16
  54.1 4.3 %copy-start.15 = (bf16[896,512]{1,0:T(8,128)(2,1)}, bf16[896,512]{1,0:T(8,128)(2,1)S(1)}, u32[]{:S(2)}) copy-start(bf16[896,512]{1,0:T(8,128)(2,1)S(1)} %constant_dynamic-update-slice_fusion.1) | copy-start | bytes 2752516
  54.1 4.3 %collective-permute-start.17 = (bf16[128,512]{1,0:T(8,128)(2,1)S(1)}, bf16[128,512]{1,0:T(8,128)(2,1)S(1)}, u32[]{:S(2)}, u32[]{:S(2)}) collective-permute-start(bf16[128,512]{1,0:T(8,128)(2,1)S(1)} %bitcast.344), channel_id=1, source_target_pairs={{0,1},{1,2},{2,3},{3,4},{4,5},{5,6},{6,7},{7,8},{8,9},{9,10},{10,1... | collective-permute-start | bytes 393224 | tf_op jit(solution)/shard_map/ppermute | solution.py:16
  58.5 3.1 %copy-start.16 = (bf16[896,512]{1,0:T(8,128)(2,1)S(1)}, bf16[896,512]{1,0:T(8,128)(2,1)}, u32[]{:S(2)}) copy-start(bf16[896,512]{1,0:T(8,128)(2,1)} %copy-done.15) | copy-start | bytes 2752516
  86.3 3.4 %copy-start.12 = (bf16[16,4,8,128]{3,2,1,0:T(8,128)(2,1)S(1)}, bf16[16,4,8,128]{3,2,1,0:T(8,128)(2,1)}, u32[]{:S(2)}) copy-start(bf16[16,4,8,128]{3,2,1,0:T(8,128)(2,1)} %get-tuple-element.11) | copy-start | bytes 393220
  98.5 3.4 %copy-start.10 = (bf16[16,4,8,128]{3,2,1,0:T(8,128)(2,1)S(1)}, bf16[16,4,8,128]{3,2,1,0:T(8,128)(2,1)}, u32[]{:S(2)}) copy-start(bf16[16,4,8,128]{3,2,1,0:T(8,128)(2,1)} %get-tuple-element.10) | copy-start | bytes 393220
  110.9 3.4 %copy-start.8 = (bf16[16,4,8,128]{3,2,1,0:T(8,128)(2,1)S(1)}, bf16[16,4,8,128]{3,2,1,0:T(8,128)(2,1)}, u32[]{:S(2)}) copy-start(bf16[16,4,8,128]{3,2,1,0:T(8,128)(2,1)} %get-tuple-element.9) | copy-start | bytes 393220
  114.3 5.1 %copy-start.17 = (bf16[896,512]{1,0:T(8,128)(2,1)S(1)}, bf16[896,512]{1,0:T(8,128)(2,1)}, u32[]{:S(2)}) copy-start(bf16[896,512]{1,0:T(8,128)(2,1)} %copy-done.15) | copy-start | bytes 2752516
  119.4 3.2 %copy-start.20 = (bf16[128,4,128]{0,2,1:T(8,128)(2,1)S(1)}, bf16[128,4,128]{0,2,1:T(8,128)(2,1)}, u32[]{:S(2)}) copy-start(bf16[128,4,128]{0,2,1:T(8,128)(2,1)} %fusion.37) | copy-start | bytes 393220
  122.5 24.7 %copy-start.3 = (f32[1,32768]{1,0:T(1,128)S(1)}, f32[1,32768]{1,0:T(1,128)}, u32[]{:S(2)}) copy-start(f32[1,32768]{1,0:T(1,128)} %param.19) | copy-start | bytes 393220
  122.8 2.1 %collective-permute-start.18 = (f32[32768]{0:T(1024)S(1)}, f32[32768]{0:T(1024)S(1)}, u32[]{:S(2)}, u32[]{:S(2)}) collective-permute-start(f32[32768]{0:T(1024)S(1)} %bitcast.321), channel_id=1, source_target_pairs={{0,1},{1,0},{2,3},{3,2},{4,5},{5,4},{6,7},{7,6},{8,9},{9,8},{10,11... | collective-permute-start | bytes 393224 | tf_op jit(solution)/shard_map/ppermute | solution.py:115
  124.9 7.6 %collective-permute-start.19 = (f32[32768]{0:T(1024)S(1)}, f32[32768]{0:T(1024)S(1)}, u32[]{:S(2)}, u32[]{:S(2)}) collective-permute-start(f32[32768]{0:T(1024)S(1)} %add.65), channel_id=1, source_target_pairs={{0,2},{1,3},{2,0},{3,1},{4,6},{5,7},{6,4},{7,5},{8,10},{9,11},{10,... | collective-permute-start | bytes 393224 | tf_op jit(solution)/shard_map/ppermute | solution.py:115
  132.5 9.0 %collective-permute-start.20 = (f32[32768]{0:T(1024)S(1)}, f32[32768]{0:T(1024)S(1)}, u32[]{:S(2)}, u32[]{:S(2)}) collective-permute-start(f32[32768]{0:T(1024)S(1)} %add.66), channel_id=1, source_target_pairs={{0,4},{1,5},{2,6},{3,7},{4,0},{5,1},{6,2},{7,3},{8,12},{9,13},{10,... | collective-permute-start | bytes 393224 | tf_op jit(solution)/shard_map/ppermute | solution.py:115
  141.5 9.3 %collective-permute-start.21 = (f32[32768]{0:T(1024)S(1)}, f32[32768]{0:T(1024)S(1)}, u32[]{:S(2)}, u32[]{:S(2)}) collective-permute-start(f32[32768]{0:T(1024)S(1)} %add.67), channel_id=1, source_target_pairs={{0,8},{1,9},{2,10},{3,11},{4,12},{5,13},{6,14},{7,15},{8,0},{9,1},... | collective-permute-start | bytes 393224 | tf_op jit(solution)/shard_map/ppermute | solution.py:115
  155.5 6.2 %copy-start.14 = (f32[1,2048]{1,0:T(1,128)}, f32[1,2048]{1,0:T(1,128)S(1)}, u32[]{:S(2)}) copy-start(f32[1,2048]{1,0:T(1,128)S(1)} %get-tuple-element.21) | copy-start | bytes 24580
